TPU v7x, 32 devices: a whole 2x2x4 slice. The times are simulated.
32 devices in a mesh: lon: 8 (over y, x, core), lat: 4 (over z).
Axes of the slice: x: 2, y: 2, z: 4, core: 2. Of those that a mesh axis runs over, the one named last changes fastest.
Arguments:
- height_old: float32 [1024, 512], P('lon', 'lat'), may hold values from -6 to 6
- height_now: float32 [1024, 512], P('lon', 'lat'), may hold values from -6 to 6
- zonal_old: float32 [1024, 512], P('lon', 'lat'), may hold values from -6 to 6
- zonal_now: float32 [1024, 512], P('lon', 'lat'), may hold values from -6 to 6
- meridional_old: float32 [1024, 512], P('lon', 'lat'), may hold values from -6 to 6
- meridional_now: float32 [1024, 512], P('lon', 'lat'), may hold values from -6 to 6
- ocean_depth: float32 [1024, 512], P('lon', 'lat'), may hold values from 0.2 to 1
- land_sea: int32 [1024, 512], P('lon', 'lat'), may hold values 0 or 1
- metric_factor: float32 [512], P('lat'), may hold values from 0.5 to 2
- coriolis: float32 [512], P('lat'), may hold values from -0.5 to 0.5
- implicit_weight: float32 [512], replicated, may hold values from 150 to 40000
- source_longitude: int32 [512], replicated, may hold values from 0 to 1023
- source_latitude: int32 [512], replicated, may hold values from 0 to 511
- source_amplitude: float32 [512], replicated, may hold values from -24 to 24
Outputs:
- height_final: float32 [1024, 512], P('lon', 'lat')
- zonal_final: float32 [1024, 512], P('lon', 'lat')
- meridional_final: float32 [1024, 512], P('lon', 'lat')
Inputs may be any that keep to these rules, and one draw needn't show every extreme that they name: `source_longitude`: cells may repeat.
All inputs are finite; a program needn't handle non-finite values. No bound on the sum of `land_sea` on one device may be relied on, other than what follows from the above.
Results may differ from a plain program's by a relative error of at most 0.0003.
Values sent between devices are 32-bit elements; how exact they have to be, the bound alone decides.
A program may use at most 64 MiB of HBM per device.

v0:
```python
import jax
import jax.numpy as jnp
from jax import lax
from jax.sharding import PartitionSpec as P

COURANT = 0.25


def extended(block, sides, width, periodic):
    for axis, dim in sides:
        count = lax.axis_size(axis)
        forward = [(i, i + 1) for i in range(count - 1)]
        if periodic:
            forward.append((count - 1, 0))
        backward = [(target, source) for source, target in forward]
        low = lax.ppermute(
            lax.slice_in_dim(block, block.shape[dim] - width, None, axis=dim), axis, forward
        )
        high = lax.ppermute(lax.slice_in_dim(block, 0, width, axis=dim), axis, backward)
        block = jnp.concatenate([low, block, high], axis=dim)
    return block


def solve_lines(lower, middle, upper, rhs):
    target = rhs.shape
    solved = lax.linalg.tridiagonal_solve(
        jnp.broadcast_to(lower, target),
        jnp.broadcast_to(middle, target),
        jnp.broadcast_to(upper, target),
        rhs[..., None],
    )
    return solved[..., 0]


def following(values):
    return jnp.concatenate([values[1:], jnp.zeros_like(values[:1])], axis=0)


def pick_row(values, index_value):
    return lax.dynamic_index_in_dim(values, index_value, 0, keepdims=False)


def per_device(
    height_old,
    height_now,
    zonal_old,
    zonal_now,
    meridional_old,
    meridional_now,
    ocean_depth,
    land_sea,
    metric_factor,
    coriolis,
    implicit_weight,
    source_longitude,
    source_latitude,
    source_amplitude,
):
    columns = height_old.shape[0]
    rows_local = height_old.shape[1]
    wetness = land_sea.astype(height_old.dtype)
    metric = metric_factor[None, :]
    turning = coriolis[None, :]
    first_east = lax.axis_index("lon") * columns
    first_north = lax.axis_index("lat") * rows_local
    east_local = source_longitude - first_east
    north_local = source_latitude - first_north
    inside = (
        (east_local >= 0) & (east_local < columns) & (north_local >= 0) & (north_local < rows_local)
    )
    east_index = jnp.clip(east_local, 0, columns - 1)
    north_index = jnp.clip(north_local, 0, rows_local - 1)
    amounts = jnp.where(inside, source_amplitude, jnp.zeros_like(source_amplitude))
    block_count = lax.axis_size("lat")
    block_index = lax.axis_index("lat")
    blocks_weight = implicit_weight.reshape(block_count, rows_local)
    inner_weight = blocks_weight[:, :-1]
    edge_weight = blocks_weight[:, -1]
    inner_count = rows_local - 1
    position = jnp.arange(inner_count)
    inner_lower = jnp.where(position[None, :] > 0, -inner_weight, jnp.zeros_like(inner_weight))
    inner_upper = jnp.where(
        position[None, :] < inner_count - 1, -inner_weight, jnp.zeros_like(inner_weight)
    )
    inner_middle = 1.0 + 2.0 * inner_weight
    unit_columns = jnp.stack([position == 0, position == inner_count - 1], axis=-1).astype(
        implicit_weight.dtype
    )
    unit_columns = jnp.broadcast_to(unit_columns, (block_count, inner_count, 2))
    responses = lax.linalg.tridiagonal_solve(inner_lower, inner_middle, inner_upper, unit_columns)
    from_below = responses[..., 0]
    from_above = responses[..., 1]
    block_ids = jnp.arange(block_count)
    link_below = jnp.where(block_ids > 0, -inner_weight[:, 0], jnp.zeros_like(edge_weight))
    link_above = -inner_weight[:, -1]
    edge_down = -edge_weight
    edge_up = jnp.where(block_ids < block_count - 1, -edge_weight, jnp.zeros_like(edge_weight))
    reduced_lower = -edge_down * link_below * from_below[:, -1]
    reduced_middle = (
        1.0
        + 2.0 * edge_weight
        - edge_down * link_above * from_above[:, -1]
        - edge_up * following(link_below) * following(from_below[:, 0])
    )
    reduced_upper = -edge_up * following(link_above) * following(from_above[:, 0])
    own_lower = pick_row(inner_lower, block_index)
    own_middle = pick_row(inner_middle, block_index)
    own_upper = pick_row(inner_upper, block_index)
    own_below = pick_row(from_below, block_index)
    own_above = pick_row(from_above, block_index)
    own_link_below = pick_row(link_below, block_index)
    own_link_above = pick_row(link_above, block_index)
    own_edge_down = pick_row(edge_down, block_index)
    flux_east = ocean_depth * wetness * zonal_now
    flux_north = ocean_depth * wetness * meridional_now
    padded_east = extended(jnp.stack([height_now, flux_east]), (("lon", 1),), 1, True)
    padded_north = extended(jnp.stack([height_now, flux_north]), (("lat", 2),), 1, False)
    across_east = padded_east[:, 2:, :] - padded_east[:, :-2, :]
    across_north = padded_north[:, :, 2:] - padded_north[:, :, :-2]
    interim = height_old - COURANT * (metric * across_east[1] + across_north[1])
    interim = interim.at[east_index, north_index].add(amounts)
    zonal_next = wetness * (
        zonal_old - COURANT * metric * across_east[0] + turning * meridional_now
    )
    meridional_next = wetness * (meridional_old - COURANT * across_north[0] - turning * zonal_now)
    partial_value = solve_lines(own_lower, own_middle, own_upper, interim[:, :-1])
    edge_rhs = interim[:, -1] - own_edge_down * partial_value[:, -1]
    packed = jnp.stack([edge_rhs, partial_value[:, 0]])[:, None, :]
    boundary = lax.all_gather(packed, "lat", axis=1, tiled=True)
    reduced_rhs = boundary[0] - edge_up[:, None] * following(boundary[1])
    separators = lax.linalg.tridiagonal_solve(
        reduced_lower, reduced_middle, reduced_upper, reduced_rhs
    )
    stacked = jnp.concatenate([jnp.zeros_like(separators[:1]), separators], axis=0)
    below_edge = pick_row(stacked, block_index)
    own_edge = pick_row(stacked, block_index + 1)
    inner_solved = (
        partial_value
        - own_link_below * below_edge[:, None] * own_below[None, :]
        - own_link_above * own_edge[:, None] * own_above[None, :]
    )
    solved = jnp.concatenate([inner_solved, own_edge[:, None]], axis=1)
    height_next = wetness * solved
    return (height_next, zonal_next, meridional_next)


def solution(mesh):
    placed = (
        P("lon", "lat"),
        P("lon", "lat"),
        P("lon", "lat"),
        P("lon", "lat"),
        P("lon", "lat"),
        P("lon", "lat"),
        P("lon", "lat"),
        P("lon", "lat"),
        P("lat"),
        P("lat"),
        P(),
        P(),
        P(),
        P(),
    )
    return jax.shard_map(
        per_device,
        mesh=mesh,
        in_specs=placed,
        out_specs=(P("lon", "lat"), P("lon", "lat"), P("lon", "lat")),
        check_vma=False,
    )
```

profile of v0, /device:TPU:0, one launch (start us, length us, event | category | flops | bytes accessed | tf_op | source)
XLA Modules:
  0.0 277.8 jit_solution(9764382970126689576)
XLA Ops:
  0.6 0.9 multiply_bitcast_fusion
  1.7 5.0 %collective-permute-start.3 = (f32[2,128,1]{2,1,0:T(8,128)S(1)}, f32[2,128,1]{2,1,0:T(8,128)S(1)}, u32[]{:S(2)}, u32[]{:S(2)}) collective-permute-start(f32[2,128,1]{2,1,0:T(8,128)S(1)} %get-tuple-element.1203), channel_id=1, source_target_pairs={{0,1},{1,2},{2,3},{4,5},{5,6},{6,7},{8,9},{9,10},{10,11},{12,13},{... | collective-permute-start | bytes 3080 | tf_op jit(solution)/shard_map/ppermute | solution.py:16
  6.7 1.3 collective-permute-start.2
  14.9 22.3 %while.66 = (s32[]{:T(128)}, f32[4]{0:T(128)S(1)}, f32[4,2]{0,1:T(2,128)S(1)}, f32[3,32,4]{1,0,2:T(4,128)S(1)}, f32[3,32,4,2]{1,0,3,2:T(4,128)S(1)}, /*index=5*/...) while((s32[]{:T(128)}, f32[4]{0:T(128)S(1)}, ...), condition=%wide.region_6.7_spmd, body=%wide.region_5.6_spmd.sunk | while | flops 1185 | bytes 18553 | solution.py:90
  50.0 12.1 %while.67 = (s32[]{:T(128)}, f32[4,2]{0,1:T(2,128)S(1)}, f32[3,32,4,2]{1,0,3,2:T(4,128)S(1)}, f32[3,32,4,2]{2,3,1,0:T(2,128)S(1)}, f32[3,32,4]{2,1,0:T(8,128)S(1...) while((s32[]{:T(128)}, f32[4,2]{0,1:T(2,128)S(1)}, ...), condition=%wide.region_8.9_spmd, body=%wide.region_7.8_spmd.sunk | while | flops 786 | bytes 14181 | solution.py:90
  79.9 2.6 collective-permute-start
  87.8 25.2 %scatter_fusion = f32[128,128]{1,0:T(8,128)S(1)} fusion(f32[128,128]{1,0:T(8,128)S(1)} %get-tuple-element.1199, s32[512]{0:T(512)S(1)} %bitcast.4527, f32[512]{0:T(512)S(1)} %and_select_fusion), kind=kCustom, calls=%fused_computation | custom fusion | flops 512 | bytes 10240 | tf_op jit(solution)/shard_map/scatter-add | solution.py:121
  113.0 0.8 fusion.736
  118.0 78.1 %while.64 = (s32[]{:T(128)}, f32[128]{0:T(128)S(1)}, f32[128,1]{0,1:T(1,128)S(1)}, f32[3,32,128]{2,1,0:T(8,128)S(1)}, f32[3,32,128,1]{2,1,3,0:T(8,128)S(1)}, /*i...) while((s32[]{:T(128)}, f32[128]{0:T(128)S(1)}, ...), condition=%wide.region_2.3_spmd, body=%wide.region_1.2_spmd.sunk | while | flops 32801 | bytes 281701 | solution.py:26
  119.5 0.8 constant_dynamic-update-slice_fusion.137
  120.3 0.8 constant_dynamic-update-slice_fusion.138
  121.1 0.8 constant_dynamic-update-slice_fusion.139
  121.9 0.8 constant_dynamic-update-slice_fusion.140
  122.7 0.8 constant_dynamic-update-slice_fusion.141
  123.5 0.8 constant_dynamic-update-slice_fusion.142
  125.0 0.8 constant_dynamic-update-slice_fusion.144
  125.9 0.8 constant_dynamic-update-slice_fusion.145
  126.7 0.8 constant_dynamic-update-slice_fusion.146
  127.5 0.8 constant_dynamic-update-slice_fusion.147
  128.3 0.8 constant_dynamic-update-slice_fusion.148
  129.2 0.8 constant_dynamic-update-slice_fusion.149
  130.0 0.8 constant_dynamic-update-slice_fusion.150
  137.8 0.8 constant_dynamic-update-slice_fusion.160
  138.6 0.8 constant_dynamic-update-slice_fusion.161
  139.4 0.8 constant_dynamic-update-slice_fusion.162
  140.3 0.8 constant_dynamic-update-slice_fusion.163
  141.1 0.8 constant_dynamic-update-slice_fusion.164
  141.9 0.8 constant_dynamic-update-slice_fusion.165
  142.7 0.8 fusion.1184
  157.6 0.8 constant_dynamic-update-slice_fusion.152
  158.4 0.8 constant_dynamic-update-slice_fusion.153
  159.2 0.8 constant_dynamic-update-slice_fusion.154
  160.0 0.8 constant_dynamic-update-slice_fusion.155
  160.8 0.8 constant_dynamic-update-slice_fusion.156
  161.5 0.8 constant_dynamic-update-slice_fusion.157
  162.3 0.8 constant_dynamic-update-slice_fusion.158
  163.9 0.8 constant_dynamic-update-slice_fusion.160
  164.7 0.8 constant_dynamic-update-slice_fusion.161
  165.5 0.8 constant_dynamic-update-slice_fusion.162
  166.2 0.8 constant_dynamic-update-slice_fusion.163
  167.0 0.8 constant_dynamic-update-slice_fusion.164
  167.8 0.8 constant_dynamic-update-slice_fusion.165
  173.3 0.8 constant_dynamic-update-slice_fusion.139
  174.1 0.8 constant_dynamic-update-slice_fusion.140
  177.2 0.8 constant_dynamic-update-slice_fusion.144
  178.0 0.8 constant_dynamic-update-slice_fusion.145
  178.8 0.8 constant_dynamic-update-slice_fusion.146
  179.6 0.8 constant_dynamic-update-slice_fusion.147
  180.4 0.8 constant_dynamic-update-slice_fusion.148
  181.2 0.8 constant_dynamic-update-slice_fusion.149
  182.0 0.8 constant_dynamic-update-slice_fusion.150
  183.5 0.8 constant_dynamic-update-slice_fusion.152
  184.3 0.8 constant_dynamic-update-slice_fusion.153
  185.1 0.8 constant_dynamic-update-slice_fusion.154
  185.9 0.8 constant_dynamic-update-slice_fusion.155
  186.7 0.8 constant_dynamic-update-slice_fusion.156
  187.5 0.8 constant_dynamic-update-slice_fusion.157
  188.3 0.8 constant_dynamic-update-slice_fusion.158
  196.2 55.7 %fusion.839 = (f32[128,1]{0,1:T(1,128)S(1)}, f32[128,1]{0,1:T(1,128)S(1)}, f32[128,1]{0,1:T(1,128)S(1)}, f32[128,1]{0,1:T(1,128)S(1)}, f32[128,1]{0,1:T(1,128)S(...) fusion(f32[128]{0:T(128)S(1)} %get-tuple-element.455, ...), kind=kLoop, calls=%fused_computation.1756 | loop fusion | flops 22912 | bytes 46948 | tf_op jit(solution)/shard_map/vmap()/eval_jaxpr/div | solution.py:26
  252.1 2.2 while.65
  258.7 0.8 fusion.731
  259.5 12.2 %all-gather = f32[2,512]{1,0:T(2,128)S(1)} all-gather(f32[2,128]{1,0:T(2,128)S(1)} %pad_maximum_fusion.10), channel_id=2, replica_groups=mesh['lon'=8,'lat'=4] {'lat'}, dimensions={1}, use_global_device_ids=true | all-gather | bytes 5120 | tf_op jit(solution)/shard_map/all_gather | solution.py:129
  273.1 1.9 subtract_divide_fusion.31
  275.6 1.3 fusion.746
  (872 shorter events, 120.7 us)
Async XLA Ops:
  0.6 1.0 copy-start
  1.7 76.7 %collective-permute-start.3 = (f32[2,128,1]{2,1,0:T(8,128)S(1)}, f32[2,128,1]{2,1,0:T(8,128)S(1)}, u32[]{:S(2)}, u32[]{:S(2)}) collective-permute-start(f32[2,128,1]{2,1,0:T(8,128)S(1)} %get-tuple-element.1203), channel_id=1, source_target_pairs={{0,1},{1,2},{2,3},{4,5},{5,6},{6,7},{8,9},{9,10},{10,11},{12,13},{... | collective-permute-start | bytes 3080 | tf_op jit(solution)/shard_map/ppermute | solution.py:16
  6.7 71.7 %collective-permute-start.2 = (f32[2,128,1]{2,1,0:T(8,128)S(1)}, f32[2,128,1]{2,1,0:T(8,128)S(1)}, u32[]{:S(2)}, u32[]{:S(2)}) collective-permute-start(f32[2,128,1]{2,1,0:T(8,128)S(1)} %get-tuple-element.1202), channel_id=1, source_target_pairs={{1,0},{2,1},{3,2},{5,4},{6,5},{7,6},{9,8},{10,9},{11,10},{13,12},{... | collective-permute-start | bytes 3080 | tf_op jit(solution)/shard_map/ppermute | solution.py:19
  8.0 0.7 copy-start.8
  69.5 0.7 copy-start.14
  70.1 0.7 copy-start.11
  70.1 0.7 copy-start.10
  70.8 0.7 copy-start.12
  78.3 0.8 copy-start.1
  78.3 0.9 copy-start.2
  78.3 0.9 copy-start.4
  78.3 0.9 copy-start.5
  78.4 0.9 copy-start.13
  79.9 6.4 %collective-permute-start.1 = (f32[2,1,128]{2,1,0:T(1,128)S(1)}, f32[2,1,128]{2,1,0:T(1,128)S(1)}, u32[]{:S(2)}, u32[]{:S(2)}) collective-permute-start(f32[2,1,128]{2,1,0:T(1,128)S(1)} %get-tuple-element.1201), channel_id=1, source_target_pairs={{0,4},{4,8},{8,12},{12,16},{16,20},{20,24},{24,28},{28,0},{1,5},{5... | collective-permute-start | bytes 3080 | tf_op jit(solution)/shard_map/ppermute | solution.py:16
  79.9 6.4 %collective-permute-start = (f32[2,1,128]{2,1,0:T(1,128)S(1)}, f32[2,1,128]{2,1,0:T(1,128)S(1)}, u32[]{:S(2)}, u32[]{:S(2)}) collective-permute-start(f32[2,1,128]{2,1,0:T(1,128)S(1)} %get-tuple-element.1200), channel_id=1, source_target_pairs={{4,0},{8,4},{12,8},{16,12},{20,16},{24,20},{28,24},{0,28},{5,1},{9... | collective-permute-start | bytes 3080 | tf_op jit(solution)/shard_map/ppermute | solution.py:19
  86.3 0.8 copy-start.3
  86.3 0.9 copy-start.6
  86.3 0.9 copy-start.7
  271.7 0.6 copy-start.9
  272.3 0.7 slice-start
where the time goes:
time: 283 us; the launch traced here: 278 us
  other arithmetic  173 us (61%)
  local copies, waits for them, and re-layouts  73.2 us (26%)
  blocking collectives  12.2 us (4%)
  starting transfers between devices  8.9 us (3%)
  between operations  8.88 us (3%)
    while x93, other arithmetic  71.5 us
    div x8, other arithmetic, solve_lines(): lax.linalg.tridiagonal_solve(jnp.broadcast_to(lower, target), jnp.broadca...  61 us
    broadcast_in_dim x379, local copies, waits for them, and re-layouts, per_device(): lax.linalg.tridiagonal_solve(inner_lower, inner_middle, inner_upper, unit...  36.4 us
    scatter-add x1, other arithmetic, per_device(): interim = interim.at[east_index, north_index].add(amounts)  25.2 us
    all_gather x1, blocking collectives, per_device(): boundary = lax.all_gather(packed, 'lat', axis=1, tiled=True)  12.2 us
    slice x46, local copies, waits for them, and re-layouts, per_device(): lax.linalg.tridiagonal_solve(inner_lower, inner_middle, inner_upper, unit...  7.91 us
    slice x14, local copies, waits for them, and re-layouts, solve_lines(): lax.linalg.tridiagonal_solve(jnp.broadcast_to(lower, target), jnp.broadca...  6.54 us
  transfers between devices with their start and end apart: 4, of which 0 were waited for; matrix products, arithmetic and copies ran while one was open for 23% of the time, Pallas kernels for 0%

commit v1 on v0

v1 whole, which is shorter than its diff:
```python
import functools

import jax
import jax.numpy as jnp
from jax import lax
from jax.experimental import pallas as pl
from jax.experimental.pallas import tpu as pltpu
from jax.sharding import PartitionSpec as P

COURANT = 0.25
MESH = pl.DeviceIdType.MESH
HIGHEST = lax.Precision.HIGHEST
LAST_WITH_LAST = (((1,), (1,)), ((), ()))
FIRST_WITH_FIRST = (((0,), (0,)), ((), ()))


def exact_dot(left, right, dims):
    return lax.dot_general(left, right, dims, precision=HIGHEST, preferred_element_type=jnp.float32)


def line_factors(weight, blocks):
    padded, rows = weight.shape
    a = 1.0 / weight
    lane = lax.broadcasted_iota(jnp.int32, (padded, rows), 1)
    one = jnp.ones_like(a)
    up = (1.0 + a, a, one, one)
    down = up
    shift = 1
    while shift < rows:

        def combined(m, amount, outside):
            o = [pltpu.roll(v, amount, 1) for v in m]
            p00 = jnp.where(outside, 1.0, o[0])
            p01 = jnp.where(outside, 0.0, o[1])
            p10 = jnp.where(outside, 0.0, o[2])
            p11 = jnp.where(outside, 1.0, o[3])
            return (
                m[0] * p00 + m[1] * p10,
                m[0] * p01 + m[1] * p11,
                m[2] * p00 + m[3] * p10,
                m[2] * p01 + m[3] * p11,
            )

        up = combined(up, shift, lane < shift)
        down = combined(down, rows - shift, lane >= rows - shift)
        shift *= 2

    def carried(m, edge, order):
        m = [jnp.broadcast_to(v[:, edge : edge + 1], (padded, rows)) for v in m]
        x, y = one[:1], jnp.zeros_like(one[:1])
        xs, ys, shrink = {}, {}, {}
        for c in order:
            xs[c], ys[c] = x, y
            nx = m[0][c : c + 1] * x + m[1][c : c + 1] * y
            ny = m[2][c : c + 1] * x + m[3][c : c + 1] * y
            ratio = 1.0 / (nx + ny)
            shrink[c] = ratio
            x, y = nx * ratio, ny * ratio
        spare = [one[:1]] * (padded - blocks)
        return [jnp.concatenate([t[c] for c in range(blocks)] + spare, axis=0) for t in (xs, ys, shrink)]

    x_in, y_in, shrink_up = carried(up, rows - 1, range(blocks))
    xb_in, yb_in, shrink_down = carried(down, 0, range(blocks - 1, -1, -1))
    x = up[0] * x_in + up[1] * y_in
    y = up[2] * x_in + up[3] * y_in
    yb = down[2] * xb_in + down[3] * yb_in
    end = lambda v: jnp.broadcast_to(v[:, rows - 1 :], (padded, rows))
    start = lambda v: jnp.broadcast_to(v[:, :1], (padded, rows))
    scale = 1.0 / (end(x) + end(y) * xb_in)
    before = COURANT * pltpu.roll(end(a), 1, 0)
    after = COURANT * pltpu.roll(start(a), padded - 1, 0)
    first = lane == 0
    last = lane == rows - 1
    zero = jnp.zeros_like(a)
    return (
        a * y,
        a * yb,
        y * scale,
        yb * scale,
        shrink_up,
        shrink_down,
        jnp.where(last, after, zero) - jnp.where(first, before * y_in * shrink_up, zero),
        jnp.where(last, after * yb_in * shrink_down, zero) - jnp.where(first, before, zero),
        -jnp.where(first, before * y_in, zero),
        jnp.where(last, after * yb_in, zero),
    )


def kernel(lons, lats, *refs):
    ins, refs = refs[:14], refs[14:]
    outs, refs = refs[:3], refs[3:]
    bufs, refs = refs[:14], refs[14:]
    (
        load_sem,
        factors,
        send_lat,
        send_side,
        send_next,
        recv_lat,
        recv_side,
        recv_next,
        lat_send_sem,
        lat_recv_sem,
        side_send_sem,
        side_recv_sem,
        next_send_sem,
        next_recv_sem,
    ) = refs
    a_id = lax.axis_index("lon")
    b_id = lax.axis_index("lat")
    sides = (lax.rem(a_id + lons - 1, lons), lax.rem(a_id + 1, lons))

    barrier = pltpu.get_barrier_semaphore()
    for k in range(1, lats):
        pl.semaphore_signal(
            barrier, inc=1, device_id=(a_id, lax.rem(b_id + k, lats)), device_id_type=MESH
        )
    for k in range(lats):
        for side in sides:
            pl.semaphore_signal(
                barrier, inc=1, device_id=(side, lax.rem(b_id + k, lats)), device_id_type=MESH
            )

    loads = [None] * 14
    for k in (10, 7, 3, 5, 6, 1, 0, 8, 11, 12, 13, 2, 4, 9):
        dst = bufs[k].at[pl.ds(0, lats)] if k == 10 else bufs[k]
        loads[k] = pltpu.make_async_copy(ins[k], dst, load_sem.at[k])
        loads[k].start()
    for load in loads:
        load.wait()
    (hold, hnow, zold, znow, mold, mnow, depth, land, met, cor, wgt, slon, slat, samp) = bufs

    columns, rows = hold.shape
    padded = wgt.shape[0]
    weight = wgt[...]
    if padded > lats:
        row_id = lax.broadcasted_iota(jnp.int32, (padded, rows), 0)
        weight = jnp.where(row_id < lats, weight, 1.0)
    for k, value in enumerate(line_factors(weight, lats)):
        factors[k] = value

    def own(k, block):
        return factors[k, pl.ds(block, 1), :]

    ay, ayb, y_s, yb_s, shrink_up, shrink_down, l_f, u_f, own_l, own_u = [
        own(k, b_id) for k in range(10)
    ]

    wet = land[...].astype(jnp.float32)
    wet_depth = depth[...] * wet
    flux_east = wet_depth * znow[...]
    flux_north = wet_depth * mnow[...]
    metric = met[...]
    line = lax.broadcasted_iota(jnp.int32, (columns, rows), 0)
    lane = lax.broadcasted_iota(jnp.int32, (columns, rows), 1)

    def inner_diff(v, axis, position, size):
        ahead = jnp.where(position == size - 1, 0.0, pltpu.roll(v, size - 1, axis))
        behind = jnp.where(position == 0, 0.0, pltpu.roll(v, 1, axis))
        return ahead - behind

    rhs = hold[...] - COURANT * (
        metric * inner_diff(flux_east, 0, line, columns) + inner_diff(flux_north, 1, lane, rows)
    )
    sources = slon.shape[1]
    east_cell = lax.broadcasted_iota(jnp.int32, (columns, sources), 0) + a_id * columns
    north_cell = lax.broadcasted_iota(jnp.int32, (rows, sources), 0) + b_id * rows
    hit_east = jnp.where(east_cell == slon[...], 1.0, 0.0).astype(jnp.bfloat16)
    hit_north = north_cell == slat[...]
    rest = samp[...]
    for _ in range(3):
        piece = rest.astype(jnp.bfloat16).astype(jnp.float32)
        rest = rest - piece
        rhs = rhs + lax.dot_general(
            hit_east,
            jnp.where(hit_north, piece, 0.0).astype(jnp.bfloat16),
            LAST_WITH_LAST,
            preferred_element_type=jnp.float32,
        )

    height = hnow[...]
    row_lane = lax.broadcasted_iota(jnp.int32, (1, rows), 1)
    first_row = jnp.where(row_lane == 0, 1.0, 0.0)
    last_row = jnp.where(row_lane == rows - 1, 1.0, 0.0)
    zero_row = jnp.zeros((1, rows), jnp.float32)
    pick = jnp.concatenate(
        [
            jnp.concatenate([ay * shrink_up, zero_row, ayb * shrink_down] + [zero_row] * 5, axis=0),
            jnp.concatenate([l_f, zero_row, u_f, zero_row, own_l, own_u, zero_row, zero_row], axis=0),
            jnp.concatenate([zero_row, last_row, zero_row, first_row] + [zero_row] * 4, axis=0),
        ],
        axis=1,
    )
    moments = exact_dot(
        pick, jnp.concatenate([rhs, flux_north, height], axis=1), LAST_WITH_LAST
    )
    send_lat[0] = moments[0:2]
    send_lat[1] = moments[2:4]
    to_west = -COURANT * metric * flux_east[0:1]
    to_east = COURANT * metric * flux_east[columns - 1 :]
    line_lane = lax.broadcasted_iota(jnp.int32, (1, columns), 1)
    for side, (row, target) in enumerate(((to_west, columns - 1), (to_east, 0))):
        for way, weights in enumerate((ay * shrink_up, ayb * shrink_down)):
            total = jnp.sum(row * weights, axis=1, keepdims=True)
            send_side[side, way] = jnp.where(line_lane == target, total, 0.0)

    pl.semaphore_wait(barrier, 3 * lats - 1)
    copies = []
    for k in range(lats - 1, 0, -1):
        target = lax.rem(b_id + k, lats)
        way = jnp.where(b_id + k < lats, 0, 1)
        for side in (0, 1):
            copies.append(
                pltpu.make_async_remote_copy(
                    src_ref=send_side.at[side, way],
                    dst_ref=recv_side.at[side, lats - k - 1],
                    send_sem=side_send_sem.at[side, k - 1],
                    recv_sem=side_recv_sem.at[side, lats - k - 1],
                    device_id=(sides[side], target),
                    device_id_type=MESH,
                )
            )
            copies[-1].start()
        copies.append(
            pltpu.make_async_remote_copy(
                src_ref=send_lat.at[way],
                dst_ref=recv_lat.at[lats - k - 1],
                send_sem=lat_send_sem.at[k - 1],
                recv_sem=lat_recv_sem.at[lats - k - 1],
                device_id=(a_id, target),
                device_id_type=MESH,
            )
        )
        copies[-1].start()

    stacked = jnp.concatenate([ay, ayb] + [zero_row] * 6, axis=0)
    columns_of = jnp.transpose(stacked)
    source_lat = lax.broadcasted_iota(jnp.int32, (rows, rows), 0)
    target_lat = lax.broadcasted_iota(jnp.int32, (rows, rows), 1)
    inverse = jnp.where(
        source_lat <= target_lat, columns_of[:, 0:1] * yb_s, columns_of[:, 1:2] * y_s
    )
    plain = (((1,), (0,)), ((), ()))
    edge_solved = exact_dot(
        jnp.concatenate([to_west, to_east] + [zero_row] * 6, axis=0), inverse, plain
    )
    send_next[0] = jnp.concatenate([height[0:1], edge_solved[0:1]], axis=0)
    send_next[1] = jnp.concatenate([height[columns - 1 :], edge_solved[1:2]], axis=0)
    for side in (0, 1):
        copies.append(
            pltpu.make_async_remote_copy(
                src_ref=send_next.at[side],
                dst_ref=recv_next.at[side],
                send_sem=next_send_sem.at[side],
                recv_sem=next_recv_sem.at[side],
                device_id=(sides[side], b_id),
                device_id_type=MESH,
            )
        )
        copies[-1].start()

    solved = exact_dot(rhs, inverse, plain)
    turning = cor[...]
    zonal_part = zold[...] + turning * mnow[...] - COURANT * metric * inner_diff(height, 0, line, columns)
    meridional_part = mold[...] - COURANT * inner_diff(height, 1, lane, rows) - turning * znow[...]
    edge_line = COURANT * metric

    growth_up, growth_down = [None] * lats, [None] * lats
    product = jnp.ones((1, rows), jnp.float32)
    for d in range(lats - 1, 0, -1):
        growth_up[d] = product
        product = product * own(4, lax.rem(b_id + d, lats))
    product = jnp.ones((1, rows), jnp.float32)
    for d in range(1, lats):
        growth_down[d] = product
        product = product * own(5, lax.rem(b_id + d, lats))

    for copy in copies:
        copy.wait()

    low, high = moments[4:5], moments[5:6]
    for d in range(1, lats):
        arrived = recv_lat[d - 1, 0:1] + recv_side[0, d - 1] + recv_side[1, d - 1]
        north = b_id + d < lats
        high = high + jnp.where(north, arrived * growth_down[d][:, :1], 0.0)
        low = low + jnp.where(north, 0.0, arrived * growth_up[d][:, :1])
    south_height = jnp.where(b_id > 0, recv_lat[lats - 2, 1:2], 0.0)
    north_height = jnp.where(b_id < lats - 1, recv_lat[0, 1:2], 0.0)
    line_zero = jnp.zeros((4, columns), jnp.float32)
    corrections = exact_dot(
        jnp.concatenate([low, high, south_height, north_height, line_zero], axis=0),
        jnp.concatenate(
            [
                jnp.concatenate([yb_s, y_s] + [zero_row] * 6, axis=0),
                jnp.concatenate(
                    [zero_row, zero_row, COURANT * first_row, -COURANT * last_row] + [zero_row] * 4,
                    axis=0,
                ),
            ],
            axis=1,
        ),
        FIRST_WITH_FIRST,
    )
    from_east, from_west = recv_next[0], recv_next[1]
    at_west, at_east = line == 0, line == columns - 1
    solved = solved + corrections[:, :rows]
    solved = solved + jnp.where(at_west, from_west[1:2], 0.0) + jnp.where(at_east, from_east[1:2], 0.0)
    outs[0][...] = wet * solved
    zonal_part = (
        zonal_part
        + jnp.where(at_west, edge_line * from_west[0:1], 0.0)
        - jnp.where(at_east, edge_line * from_east[0:1], 0.0)
    )
    outs[1][...] = wet * zonal_part
    outs[2][...] = wet * (meridional_part + corrections[:, rows:])


def per_device(lons, lats, *args):
    args = list(args)
    columns, rows = args[0].shape
    sources = args[11].shape[0]
    padded = -(-lats // 8) * 8
    args[8] = args[8].reshape(1, rows)
    args[9] = args[9].reshape(1, rows)
    args[10] = args[10].reshape(lats, rows)
    for k in (11, 12, 13):
        args[k] = args[k].reshape(1, sources)
    shapes = [a.shape for a in args]
    shapes[10] = (padded, rows)
    out = jax.ShapeDtypeStruct((columns, rows), jnp.float32)
    others = lats - 1
    return pl.pallas_call(
        functools.partial(kernel, lons, lats),
        out_shape=(out, out, out),
        in_specs=[pl.BlockSpec(memory_space=pl.ANY)] * 14,
        out_specs=(pl.BlockSpec(memory_space=pltpu.VMEM),) * 3,
        scratch_shapes=[pltpu.VMEM(s, a.dtype) for s, a in zip(shapes, args)]
        + [
            pltpu.SemaphoreType.DMA((14,)),
            pltpu.VMEM((10, padded, rows), jnp.float32),
            pltpu.VMEM((2, 2, columns), jnp.float32),
            pltpu.VMEM((2, 2, 1, columns), jnp.float32),
            pltpu.VMEM((2, 2, rows), jnp.float32),
            pltpu.VMEM((others, 2, columns), jnp.float32),
            pltpu.VMEM((2, others, 1, columns), jnp.float32),
            pltpu.VMEM((2, 2, rows), jnp.float32),
            pltpu.SemaphoreType.DMA((others,)),
            pltpu.SemaphoreType.DMA((others,)),
            pltpu.SemaphoreType.DMA((2, others)),
            pltpu.SemaphoreType.DMA((2, others)),
            pltpu.SemaphoreType.DMA((2,)),
            pltpu.SemaphoreType.DMA((2,)),
        ],
        compiler_params=pltpu.CompilerParams(collective_id=0, has_side_effects=True),
    )(*args)


def solution(mesh):
    field = P("lon", "lat")
    placed = (field,) * 8 + (P("lat"),) * 2 + (P(),) * 4
    return jax.shard_map(
        functools.partial(per_device, mesh.shape["lon"], mesh.shape["lat"]),
        mesh=mesh,
        in_specs=placed,
        out_specs=(field,) * 3,
        check_vma=False,
    )
```

time: 283 us -> 15.7 us (0.06); the launches traced: 278 us -> 15.5 us
  other arithmetic: 173 us -> 0 us
  local copies, waits for them, and re-layouts: 73.2 us -> 3 us
  blocking collectives: 12.2 us -> 0 us
  Pallas kernels: 0 us -> 11.8 us
  starting transfers between devices: 8.9 us -> 0 us
  between operations: 8.88 us -> 0.65 us
    while x93 -> x0, other arithmetic: 71.5 us -> none
    div x18 -> x0, other arithmetic: 65.9 us -> none  [the longest x8 61 us: solve_lines(): lax.linalg.tridiagonal_solve(jnp.broadcast_to(lower, target), jnp.broadca...]
    broadcast_in_dim x413 -> x0, local copies, waits for them, and re-layouts: 40 us -> none  [the longest x379 36.4 us: per_device(): lax.linalg.tridiagonal_solve(inner_lower, inner_middle, inner_upper, unit...]
    scatter-add x1 -> x0, other arithmetic: 25.2 us -> none  [per_device(): interim = interim.at[east_index, north_index].add(amounts)]
    slice x72 -> x0, local copies, waits for them, and re-layouts: 17.8 us -> none  [the longest x46 7.91 us: per_device(): lax.linalg.tridiagonal_solve(inner_lower, inner_middle, inner_upper, unit...]
    all_gather x1 -> x0, blocking collectives: 12.2 us -> none  [per_device(): boundary = lax.all_gather(packed, 'lat', axis=1, tiled=True)]
    pallas_call x0 -> x1, Pallas kernels: none -> 11.8 us  [per_device(): pl.pallas_call(functools.partial(kernel, lons, lats), out_shape=(out, out...]
    ppermute x4 -> x0, starting transfers between devices: 8.9 us -> none  [the longest x2 4.97 us: extended(): lax.ppermute(lax.slice_in_dim(block, block.shape[dim] - width, None, axis...]
  transfers between devices with their start and end apart: 4 -> 0, of which waited for: 0 -> 0; matrix products, arithmetic and copies ran while one was open for 23% -> 0% of each run, Pallas kernels for 0% -> 0%
where the time goes in v1:
time: 15.7 us; the launch traced here: 15.5 us
  Pallas kernels  11.8 us (75%)
  local copies, waits for them, and re-layouts  3 us (19%)
  between operations  0.65 us (4%)
    pallas_call x1, Pallas kernels, per_device(): pl.pallas_call(functools.partial(kernel, lons, lats), out_shape=(out, out...  11.8 us
    unnamed x7, local copies, waits for them, and re-layouts  3 us

profile of v1, /device:TPU:0, one launch (start us, length us, event | category | flops | bytes accessed | tf_op | source)
XLA Modules:
  0.0 15.5 jit_solution(15191426553699604038)
XLA Ops:
  0.6 11.8 %shard_map.157 = (f32[128,128]{1,0:T(8,128)}, f32[128,128]{1,0:T(8,128)}, f32[128,128]{1,0:T(8,128)}) custom-call(f32[128,128]{1,0:T(8,128)} %refs_0_.1, f32[128,128]{1,0:T(8,128)} %refs_1_.1, f32[128,128]{1,0:T(8,128)} %refs_2_.1, f32[128,128]{1,0:T(8,128)} %refs_3_.1, f32[128,128]{1,0:T(8,128)} %refs_4_.1, f32[128,128]{1,0:T(8,128)} %refs_5_.1, ...), custom_call_target="tpu_custom_call" | custom-call | tf_op jit(solution)/shard_map/pallas_call | solution.py:332
  12.4 0.0 copy-start.1
  12.5 1.5 %copy.20 = f32[128,128]{1,0:T(8,128)} copy(f32[128,128]{1,0:T(8,128)} %get-tuple-element.6) | data formatting | bytes 131072
  14.0 0.0 copy-done.1
  14.0 0.0 copy-start
  14.0 0.6 %copy.21 = f32[128,128]{1,0:T(8,128)} copy(f32[128,128]{1,0:T(8,128)S(1)} %copy-done.1) | data formatting | bytes 131072
  14.6 0.2 %copy-done = f32[128,128]{1,0:T(8,128)S(1)} copy-done((f32[128,128]{1,0:T(8,128)S(1)}, f32[128,128]{1,0:T(8,128)}, u32[]{:S(2)}) %copy-start) | copy-done | bytes 65560
  14.8 0.6 %copy.22 = f32[128,128]{1,0:T(8,128)} copy(f32[128,128]{1,0:T(8,128)S(1)} %copy-done) | data formatting | bytes 131072
Async XLA Ops:
  12.4 1.5 %copy-start.1 = (f32[128,128]{1,0:T(8,128)S(1)}, f32[128,128]{1,0:T(8,128)}, u32[]{:S(2)}) copy-start(f32[128,128]{1,0:T(8,128)} %get-tuple-element.7) | copy-start | bytes 196612
  14.0 0.9 %copy-start = (f32[128,128]{1,0:T(8,128)S(1)}, f32[128,128]{1,0:T(8,128)}, u32[]{:S(2)}) copy-start(f32[128,128]{1,0:T(8,128)} %get-tuple-element.8) | copy-start | bytes 196612

commit v2 on v1

--- a/solution.py
+++ b/solution.py
@@ -315,6 +315,16 @@
     outs[2][...] = wet * (meridional_part + corrections[:, rows:])
 
 
+def store_kernel(*refs):
+    stores = [
+        pltpu.make_async_copy(refs[k], refs[3 + k], refs[6].at[k]) for k in range(3)
+    ]
+    for store in stores:
+        store.start()
+    for store in stores:
+        store.wait()
+
+
 def per_device(lons, lats, *args):
     args = list(args)
     columns, rows = args[0].shape
@@ -327,9 +337,9 @@
         args[k] = args[k].reshape(1, sources)
     shapes = [a.shape for a in args]
     shapes[10] = (padded, rows)
-    out = jax.ShapeDtypeStruct((columns, rows), jnp.float32)
+    out = pltpu.VMEM((columns, rows), jnp.float32)
     others = lats - 1
-    return pl.pallas_call(
+    results = pl.pallas_call(
         functools.partial(kernel, lons, lats),
         out_shape=(out, out, out),
         in_specs=[pl.BlockSpec(memory_space=pl.ANY)] * 14,
@@ -353,6 +363,13 @@
         ],
         compiler_params=pltpu.CompilerParams(collective_id=0, has_side_effects=True),
     )(*args)
+    return pl.pallas_call(
+        store_kernel,
+        out_shape=(jax.ShapeDtypeStruct((columns, rows), jnp.float32),) * 3,
+        in_specs=[pl.BlockSpec(memory_space=pltpu.VMEM)] * 3,
+        out_specs=(pl.BlockSpec(memory_space=pl.ANY),) * 3,
+        scratch_shapes=[pltpu.SemaphoreType.DMA((3,))],
+    )(*[pltpu.with_memory_space_constraint(r, pltpu.VMEM) for r in results])
 
 
 def solution(mesh):

time: 15.7 us -> 12.7 us (0.81)
  local copies, waits for them, and re-layouts: 3 us -> 0 us
    unnamed x7 -> x0, local copies, waits for them, and re-layouts: 3 us -> none
    pallas_call x0 -> x1, Pallas kernels: none -> 0.7 us  [per_device(): pl.pallas_call(store_kernel, out_shape=(jax.ShapeDtypeStruct((columns, ro...]
    pallas_call x1, Pallas kernels: 11.8 us -> 11.2 us  [per_device(): pl.pallas_call(functools.partial(kernel, lons, lats), out_shape=(out, out...]
where the time goes in v2:
time: 12.7 us; the launch traced here: 12.5 us
  Pallas kernels  11.9 us (94%)
  between operations  0.64 us (5%)
    pallas_call x1, Pallas kernels, per_device(): pl.pallas_call(functools.partial(kernel, lons, lats), out_shape=(out, out...  11.2 us
    pallas_call x1, Pallas kernels, per_device(): pl.pallas_call(store_kernel, out_shape=(jax.ShapeDtypeStruct((columns, ro...  0.7 us

profile of v2, /device:TPU:0, one launch (start us, length us, event | category | flops | bytes accessed | tf_op | source)
XLA Modules:
  0.0 12.5 jit_solution(3814830700891019468)
XLA Ops:
  0.6 11.2 %shard_map.157 = (f32[128,128]{1,0:T(8,128)S(1)}, f32[128,128]{1,0:T(8,128)S(1)}, f32[128,128]{1,0:T(8,128)S(1)}) custom-call(f32[128,128]{1,0:T(8,128)} %refs_0_.1, f32[128,128]{1,0:T(8,128)} %refs_1_.1, f32[128,128]{1,0:T(8,128)} %refs_2_.1, f32[128,128]{1,0:T(8,128)} %refs_3_.1, f32[128,128]{1,0:T(8,128)} %refs_4_.1, f32[128,128]{1,0:T(8,128)} %refs_5_.1, ...), custom_call_target="tpu_custom_call" | custom-call | tf_op jit(solution)/shard_map/pallas_call | solution.py:342
  11.8 0.7 %shard_map.158 = (f32[128,128]{1,0:T(8,128)}, f32[128,128]{1,0:T(8,128)}, f32[128,128]{1,0:T(8,128)}) custom-call(f32[128,128]{1,0:T(8,128)S(1)} %get-tuple-element.6.refs_0_, f32[128,128]{1,0:T(8,128)S(1)} %get-tuple-element.7.refs_1_, f32[128,128]{1,0:T(8,128)S(1)} %get-tuple-element.8.refs_2_), custom_call_target="tpu_custom_call" | custom-call | tf_op jit(solution)/shard_map/pallas_call | solution.py:366

commit v3 on v2

--- a/solution.py
+++ b/solution.py
@@ -111,33 +111,71 @@
     sides = (lax.rem(a_id + lons - 1, lons), lax.rem(a_id + 1, lons))
 
     barrier = pltpu.get_barrier_semaphore()
+    loads = [
+        pltpu.make_async_copy(
+            ins[k], bufs[k].at[pl.ds(0, lats)] if k == 10 else bufs[k], load_sem.at[k]
+        )
+        for k in range(14)
+    ]
+    early, late = (3, 6, 7, 8, 1, 10), (5, 0, 11, 12, 13, 2, 4, 9)
+    for side in sides:
+        pl.semaphore_signal(barrier, inc=1, device_id=(side, b_id), device_id_type=MESH)
+    for k in early + late:
+        loads[k].start()
     for k in range(1, lats):
-        pl.semaphore_signal(
-            barrier, inc=1, device_id=(a_id, lax.rem(b_id + k, lats)), device_id_type=MESH
-        )
-    for k in range(lats):
-        for side in sides:
-            pl.semaphore_signal(
-                barrier, inc=1, device_id=(side, lax.rem(b_id + k, lats)), device_id_type=MESH
-            )
-
-    loads = [None] * 14
-    for k in (10, 7, 3, 5, 6, 1, 0, 8, 11, 12, 13, 2, 4, 9):
-        dst = bufs[k].at[pl.ds(0, lats)] if k == 10 else bufs[k]
-        loads[k] = pltpu.make_async_copy(ins[k], dst, load_sem.at[k])
-        loads[k].start()
-    for load in loads:
-        load.wait()
+        other = lax.rem(b_id + k, lats)
+        for column in (*sides, a_id):
+            pl.semaphore_signal(barrier, inc=1, device_id=(column, other), device_id_type=MESH)
     (hold, hnow, zold, znow, mold, mnow, depth, land, met, cor, wgt, slon, slat, samp) = bufs
-
     columns, rows = hold.shape
     padded = wgt.shape[0]
+    for k in early:
+        loads[k].wait()
+
+    scaled_metric = COURANT * met[...]
+    for side, (at, sign) in enumerate(((0, -1.0), (columns - 1, 1.0))):
+        edge = pl.ds(at, 1)
+        flux = depth[edge, :] * land[edge, :].astype(jnp.float32) * znow[edge, :]
+        flux = sign * scaled_metric * flux
+        send_side[side] = flux
+        send_next[side] = jnp.concatenate([flux, hnow[edge, :]], axis=0)
+
     weight = wgt[...]
     if padded > lats:
         row_id = lax.broadcasted_iota(jnp.int32, (padded, rows), 0)
         weight = jnp.where(row_id < lats, weight, 1.0)
     for k, value in enumerate(line_factors(weight, lats)):
         factors[k] = value
+
+    pl.semaphore_wait(barrier, 3 * lats - 1)
+    side_copies, copies = [], []
+    for k in range(lats - 1, 0, -1):
+        for side in (0, 1):
+            side_copies.append(
+                pltpu.make_async_remote_copy(
+                    src_ref=send_side.at[side],
+                    dst_ref=recv_side.at[side, lats - k - 1],
+                    send_sem=side_send_sem.at[side, k - 1],
+                    recv_sem=side_recv_sem.at[side, lats - k - 1],
+                    device_id=(sides[side], lax.rem(b_id + k, lats)),
+                    device_id_type=MESH,
+                )
+            )
+            side_copies[-1].start()
+    for side in (0, 1):
+        copies.append(
+            pltpu.make_async_remote_copy(
+                src_ref=send_next.at[side],
+                dst_ref=recv_next.at[side],
+                send_sem=next_send_sem.at[side],
+                recv_sem=next_recv_sem.at[side],
+                device_id=(sides[side], b_id),
+                device_id_type=MESH,
+            )
+        )
+        copies[-1].start()
+    for k in late:
+        loads[k].wait()
 
     def own(k, block):
         return factors[k, pl.ds(block, 1), :]
@@ -196,38 +234,14 @@
     )
     send_lat[0] = moments[0:2]
     send_lat[1] = moments[2:4]
-    to_west = -COURANT * metric * flux_east[0:1]
-    to_east = COURANT * metric * flux_east[columns - 1 :]
-    line_lane = lax.broadcasted_iota(jnp.int32, (1, columns), 1)
-    for side, (row, target) in enumerate(((to_west, columns - 1), (to_east, 0))):
-        for way, weights in enumerate((ay * shrink_up, ayb * shrink_down)):
-            total = jnp.sum(row * weights, axis=1, keepdims=True)
-            send_side[side, way] = jnp.where(line_lane == target, total, 0.0)
-
-    pl.semaphore_wait(barrier, 3 * lats - 1)
-    copies = []
     for k in range(lats - 1, 0, -1):
-        target = lax.rem(b_id + k, lats)
-        way = jnp.where(b_id + k < lats, 0, 1)
-        for side in (0, 1):
-            copies.append(
-                pltpu.make_async_remote_copy(
-                    src_ref=send_side.at[side, way],
-                    dst_ref=recv_side.at[side, lats - k - 1],
-                    send_sem=side_send_sem.at[side, k - 1],
-                    recv_sem=side_recv_sem.at[side, lats - k - 1],
-                    device_id=(sides[side], target),
-                    device_id_type=MESH,
-                )
-            )
-            copies[-1].start()
         copies.append(
             pltpu.make_async_remote_copy(
-                src_ref=send_lat.at[way],
+                src_ref=send_lat.at[jnp.where(b_id + k < lats, 0, 1)],
                 dst_ref=recv_lat.at[lats - k - 1],
                 send_sem=lat_send_sem.at[k - 1],
                 recv_sem=lat_recv_sem.at[lats - k - 1],
-                device_id=(a_id, target),
+                device_id=(a_id, lax.rem(b_id + k, lats)),
                 device_id_type=MESH,
             )
         )
@@ -241,49 +255,35 @@
         source_lat <= target_lat, columns_of[:, 0:1] * yb_s, columns_of[:, 1:2] * y_s
     )
     plain = (((1,), (0,)), ((), ()))
-    edge_solved = exact_dot(
-        jnp.concatenate([to_west, to_east] + [zero_row] * 6, axis=0), inverse, plain
-    )
-    send_next[0] = jnp.concatenate([height[0:1], edge_solved[0:1]], axis=0)
-    send_next[1] = jnp.concatenate([height[columns - 1 :], edge_solved[1:2]], axis=0)
-    for side in (0, 1):
-        copies.append(
-            pltpu.make_async_remote_copy(
-                src_ref=send_next.at[side],
-                dst_ref=recv_next.at[side],
-                send_sem=next_send_sem.at[side],
-                recv_sem=next_recv_sem.at[side],
-                device_id=(sides[side], b_id),
-                device_id_type=MESH,
-            )
-        )
-        copies[-1].start()
-
     solved = exact_dot(rhs, inverse, plain)
     turning = cor[...]
     zonal_part = zold[...] + turning * mnow[...] - COURANT * metric * inner_diff(height, 0, line, columns)
     meridional_part = mold[...] - COURANT * inner_diff(height, 1, lane, rows) - turning * znow[...]
-    edge_line = COURANT * metric
-
-    growth_up, growth_down = [None] * lats, [None] * lats
-    product = jnp.ones((1, rows), jnp.float32)
+
+    growth, reach = [None] * lats, [None] * lats
+    up_product = jnp.ones((1, rows), jnp.float32)
     for d in range(lats - 1, 0, -1):
-        growth_up[d] = product
-        product = product * own(4, lax.rem(b_id + d, lats))
-    product = jnp.ones((1, rows), jnp.float32)
+        block = lax.rem(b_id + d, lats)
+        growth[d] = up_product
+        up_product = up_product * own(4, block)
+        reach[d] = own(0, block) * up_product
+    down_product = jnp.ones((1, rows), jnp.float32)
     for d in range(1, lats):
-        growth_down[d] = product
-        product = product * own(5, lax.rem(b_id + d, lats))
+        block = lax.rem(b_id + d, lats)
+        north = b_id + d < lats
+        growth[d] = jnp.where(north, down_product, growth[d])
+        down_product = down_product * own(5, block)
+        reach[d] = jnp.where(north, own(1, block) * down_product, reach[d])
 
     for copy in copies:
         copy.wait()
 
     low, high = moments[4:5], moments[5:6]
     for d in range(1, lats):
-        arrived = recv_lat[d - 1, 0:1] + recv_side[0, d - 1] + recv_side[1, d - 1]
+        arrived = recv_lat[d - 1, 0:1] * growth[d][:, :1]
         north = b_id + d < lats
-        high = high + jnp.where(north, arrived * growth_down[d][:, :1], 0.0)
-        low = low + jnp.where(north, 0.0, arrived * growth_up[d][:, :1])
+        high = high + jnp.where(north, arrived, 0.0)
+        low = low + jnp.where(north, 0.0, arrived)
     south_height = jnp.where(b_id > 0, recv_lat[lats - 2, 1:2], 0.0)
     north_height = jnp.where(b_id < lats - 1, recv_lat[0, 1:2], 0.0)
     line_zero = jnp.zeros((4, columns), jnp.float32)
@@ -302,17 +302,40 @@
         FIRST_WITH_FIRST,
     )
     from_east, from_west = recv_next[0], recv_next[1]
+    edge_solved = exact_dot(
+        jnp.concatenate([from_west[0:1], from_east[0:1]] + [zero_row] * 6, axis=0), inverse, plain
+    )
     at_west, at_east = line == 0, line == columns - 1
     solved = solved + corrections[:, :rows]
-    solved = solved + jnp.where(at_west, from_west[1:2], 0.0) + jnp.where(at_east, from_east[1:2], 0.0)
     outs[0][...] = wet * solved
     zonal_part = (
         zonal_part
-        + jnp.where(at_west, edge_line * from_west[0:1], 0.0)
-        - jnp.where(at_east, edge_line * from_east[0:1], 0.0)
+        + jnp.where(at_west, scaled_metric * from_west[1:2], 0.0)
+        - jnp.where(at_east, scaled_metric * from_east[1:2], 0.0)
     )
     outs[1][...] = wet * zonal_part
     outs[2][...] = wet * (meridional_part + corrections[:, rows:])
+
+    for copy in side_copies:
+        copy.wait()
+    terms = []
+    for side in (1, 0):
+        low, high = zero_row, zero_row
+        for d in range(1, lats):
+            arrived = recv_side[side, d - 1] * reach[d]
+            north = b_id + d < lats
+            high = high + jnp.where(north, arrived, 0.0)
+            low = low + jnp.where(north, 0.0, arrived)
+        terms += [low, high]
+    sums = jnp.sum(jnp.concatenate(terms + [zero_row] * 4, axis=0), axis=1, keepdims=True)
+    for k, at in enumerate((0, columns - 1)):
+        edge = pl.ds(at, 1)
+        outs[0][edge, :] = wet[at : at + 1] * (
+            solved[at : at + 1]
+            + edge_solved[k : k + 1]
+            + sums[2 * k : 2 * k + 1] * yb_s
+            + sums[2 * k + 1 : 2 * k + 2] * y_s
+        )
 
 
 def store_kernel(*refs):
@@ -349,10 +372,10 @@
             pltpu.SemaphoreType.DMA((14,)),
             pltpu.VMEM((10, padded, rows), jnp.float32),
             pltpu.VMEM((2, 2, columns), jnp.float32),
-            pltpu.VMEM((2, 2, 1, columns), jnp.float32),
+            pltpu.VMEM((2, 1, rows), jnp.float32),
             pltpu.VMEM((2, 2, rows), jnp.float32),
             pltpu.VMEM((others, 2, columns), jnp.float32),
-            pltpu.VMEM((2, others, 1, columns), jnp.float32),
+            pltpu.VMEM((2, others, 1, rows), jnp.float32),
             pltpu.VMEM((2, 2, rows), jnp.float32),
             pltpu.SemaphoreType.DMA((others,)),
             pltpu.SemaphoreType.DMA((others,)),

time: 12.7 us -> 12.1 us (0.953)
  Pallas kernels: 11.9 us -> 11.2 us
    pallas_call x1, Pallas kernels: 11.2 us -> 10.5 us  [per_device(): pl.pallas_call(functools.partial(kernel, lons, lats), out_shape=(out, out...]
where the time goes in v3:
time: 12.1 us; the launch traced here: 11.9 us
  Pallas kernels  11.2 us (93%)
  between operations  0.64 us (5%)
    pallas_call x1, Pallas kernels, per_device(): pl.pallas_call(functools.partial(kernel, lons, lats), out_shape=(out, out...  10.5 us
    pallas_call x1, Pallas kernels, per_device(): pl.pallas_call(store_kernel, out_shape=(jax.ShapeDtypeStruct((columns, ro...  0.7 us

profile of v3, /device:TPU:0, one launch (start us, length us, event | category | flops | bytes accessed | tf_op | source)
XLA Modules:
  0.0 11.9 jit_solution(10400449924751094400)
XLA Ops:
  0.6 10.5 %shard_map.157 = (f32[128,128]{1,0:T(8,128)S(1)}, f32[128,128]{1,0:T(8,128)S(1)}, f32[128,128]{1,0:T(8,128)S(1)}) custom-call(f32[128,128]{1,0:T(8,128)} %refs_0_.1, f32[128,128]{1,0:T(8,128)} %refs_1_.1, f32[128,128]{1,0:T(8,128)} %refs_2_.1, f32[128,128]{1,0:T(8,128)} %refs_3_.1, f32[128,128]{1,0:T(8,128)} %refs_4_.1, f32[128,128]{1,0:T(8,128)} %refs_5_.1, ...), custom_call_target="tpu_custom_call" | custom-call | tf_op jit(solution)/shard_map/pallas_call | solution.py:365
  11.2 0.7 %shard_map.158 = (f32[128,128]{1,0:T(8,128)}, f32[128,128]{1,0:T(8,128)}, f32[128,128]{1,0:T(8,128)}) custom-call(f32[128,128]{1,0:T(8,128)S(1)} %get-tuple-element.6.refs_0_, f32[128,128]{1,0:T(8,128)S(1)} %get-tuple-element.7.refs_1_, f32[128,128]{1,0:T(8,128)S(1)} %get-tuple-element.8.refs_2_), custom_call_target="tpu_custom_call" | custom-call | tf_op jit(solution)/shard_map/pallas_call | solution.py:389

commit v4 on v3

--- a/solution.py
+++ b/solution.py
@@ -117,10 +117,10 @@
         )
         for k in range(14)
     ]
-    early, late = (3, 6, 7, 8, 1, 10), (5, 0, 11, 12, 13, 2, 4, 9)
+    early, late = (3, 6, 7, 8, 1), (5, 0, 11, 12, 13, 2, 4, 9)
     for side in sides:
         pl.semaphore_signal(barrier, inc=1, device_id=(side, b_id), device_id_type=MESH)
-    for k in early + late:
+    for k in (*early, 10, *late):
         loads[k].start()
     for k in range(1, lats):
         other = lax.rem(b_id + k, lats)
@@ -139,13 +139,6 @@
         flux = sign * scaled_metric * flux
         send_side[side] = flux
         send_next[side] = jnp.concatenate([flux, hnow[edge, :]], axis=0)
-
-    weight = wgt[...]
-    if padded > lats:
-        row_id = lax.broadcasted_iota(jnp.int32, (padded, rows), 0)
-        weight = jnp.where(row_id < lats, weight, 1.0)
-    for k, value in enumerate(line_factors(weight, lats)):
-        factors[k] = value
 
     pl.semaphore_wait(barrier, 3 * lats - 1)
     side_copies, copies = [], []
@@ -174,6 +167,14 @@
             )
         )
         copies[-1].start()
+    loads[10].wait()
+    weight = wgt[...]
+    if padded > lats:
+        row_id = lax.broadcasted_iota(jnp.int32, (padded, rows), 0)
+        weight = jnp.where(row_id < lats, weight, 1.0)
+    for k, value in enumerate(line_factors(weight, lats)):
+        factors[k] = value
+
     for k in late:
         loads[k].wait()
 

time: 12.1 us -> 12.7 us (1.050)
  Pallas kernels: 11.2 us -> 11.9 us
    pallas_call x1, Pallas kernels: 10.5 us -> 11.2 us  [per_device(): pl.pallas_call(functools.partial(kernel, lons, lats), out_shape=(out, out...]
where the time goes in v4:
time: 12.7 us; the launch traced here: 12.6 us
  Pallas kernels  11.9 us (94%)
  between operations  0.64 us (5%)
    pallas_call x1, Pallas kernels, per_device(): pl.pallas_call(functools.partial(kernel, lons, lats), out_shape=(out, out...  11.2 us
    pallas_call x1, Pallas kernels, per_device(): pl.pallas_call(store_kernel, out_shape=(jax.ShapeDtypeStruct((columns, ro...  0.7 us

profile of v4, /device:TPU:0, one launch (start us, length us, event | category | flops | bytes accessed | tf_op | source)
XLA Modules:
  0.0 12.6 jit_solution(10075938828081336861)
XLA Ops:
  0.6 11.2 %shard_map.157 = (f32[128,128]{1,0:T(8,128)S(1)}, f32[128,128]{1,0:T(8,128)S(1)}, f32[128,128]{1,0:T(8,128)S(1)}) custom-call(f32[128,128]{1,0:T(8,128)} %refs_0_.1, f32[128,128]{1,0:T(8,128)} %refs_1_.1, f32[128,128]{1,0:T(8,128)} %refs_2_.1, f32[128,128]{1,0:T(8,128)} %refs_3_.1, f32[128,128]{1,0:T(8,128)} %refs_4_.1, f32[128,128]{1,0:T(8,128)} %refs_5_.1, ...), custom_call_target="tpu_custom_call" | custom-call | tf_op jit(solution)/shard_map/pallas_call | solution.py:366
  11.9 0.7 %shard_map.158 = (f32[128,128]{1,0:T(8,128)}, f32[128,128]{1,0:T(8,128)}, f32[128,128]{1,0:T(8,128)}) custom-call(f32[128,128]{1,0:T(8,128)S(1)} %get-tuple-element.6.refs_0_, f32[128,128]{1,0:T(8,128)S(1)} %get-tuple-element.7.refs_1_, f32[128,128]{1,0:T(8,128)S(1)} %get-tuple-element.8.refs_2_), custom_call_target="tpu_custom_call" | custom-call | tf_op jit(solution)/shard_map/pallas_call | solution.py:390
